TPU v7x, 32 devices: a whole 2x2x4 slice. The times are simulated.
32 devices in a mesh: seq: 8 (over z, core), ch: 4 (over y, x).
Axes of the slice: x: 2, y: 2, z: 4, core: 2. Of those that a mesh axis runs over, the one named last changes fastest.
Arguments:
- input_q: bfloat16 [4096, 8192], P('seq', 'ch'), may hold values from -6 to 6
- input_k: bfloat16 [4096, 8192], P('seq', 'ch'), may hold values from -6 to 6
- input_v: bfloat16 [4096, 8192], P('seq', 'ch'), may hold values from -6 to 6
- grad_out: bfloat16 [4096, 8192], P('seq', 'ch'), may hold values from -6 to 6
- short_filters: float32 [3, 3, 8192], P(None, None, 'ch'), may hold values from -3.5 to 3.5
- long_filter: float32 [128, 8192], P(None, 'ch'), may hold values from -0.5 to 0.5
- skip_gain: float32 [8192], P('ch'), may hold values from 0.5 to 1.5
Outputs:
- grad_input_q: bfloat16 [4096, 8192], P('seq', 'ch')
- grad_input_k: bfloat16 [4096, 8192], P('seq', 'ch')
- grad_input_v: bfloat16 [4096, 8192], P('seq', 'ch')
- grad_long: float32 [128, 8192], P('seq', 'ch')
- grad_short: float32 [3, 3, 8192], P(None, None, 'ch')
- grad_skip: float32 [8192], P('ch')
All inputs are finite; a program needn't handle non-finite values.
Results may differ from a plain program's by a relative error of at most 0.001.
Values may be sent and summed in bfloat16 or wider, within the bound.
A program may use at most 128 MiB of HBM per device.

v0:
```python
import functools

import jax
import jax.numpy as jnp
import numpy as np
from jax import lax
from jax.experimental import pallas as pl
from jax.experimental.pallas import tpu as pltpu
from jax.sharding import PartitionSpec as P

F32 = jnp.float32
BF16 = jnp.bfloat16
ROWS = 16


def shifted(value, axis, by):
    size = lax.axis_size(axis)
    pairs = [(i, i + by) for i in range(size) if 0 <= i + by < size]
    return lax.ppermute(value, axis, pairs)


def transforms(span):
    freq = np.concatenate([np.arange(0, span, 2), np.arange(1, span, 2)]) + 0.5
    angle = np.pi * np.outer(freq, np.arange(span)) / span
    fwd = np.concatenate([np.cos(angle), -np.sin(angle)], 0)
    inv = fwd.T / span

    def halves(mat):
        mat = mat.astype(np.float32)
        high = mat.astype(jnp.bfloat16)
        low = (mat - high.astype(np.float32)).astype(jnp.bfloat16)
        return high, low

    fh, fl = halves(fwd)
    ih, il = halves(inv)
    return (
        np.concatenate([fh, fh], 1),
        fl,
        ih,
        il,
    )


def split(value):
    high = value.astype(BF16)
    low = (value - high.astype(F32)).astype(BF16)
    return high, low


def down(window, by, rows):
    return pltpu.roll(window, by, 0)[8 : 8 + rows]


def up(window, by, rows):
    return pltpu.roll(window, rows + 8 - by, 0)[:rows]


def kernel(
    length, span, ntap, pad,
    q_ref, k_ref, v_ref, g_ref, kp_ref, vp_ref, qp_ref, qn_ref, gn_ref, kn_ref, vn_ref,
    sf_ref, lf_ref, hr_ref, gain_ref, fh_ref, fl_ref, ih_ref, il_ref,
    bq_ref, bk_ref, bv_ref, part_ref,
    qx, kx, vx, gx, kf, vf, zf, gs, zs, gss, zw, gw, hw, acc, sx, gz, prod,
):
    width = q_ref.shape[1]
    half = span // 2
    nblk = length // span
    big = span + pad
    kx[:big] = kp_ref[...].astype(F32)
    kx[big : big + length] = k_ref[...].astype(F32)
    kx[big + length :] = kn_ref[...].astype(F32)
    vx[:big] = vp_ref[...].astype(F32)
    vx[big : big + length] = v_ref[...].astype(F32)
    vx[big + length :] = vn_ref[...].astype(F32)
    qx[:pad] = qp_ref[...].astype(F32)
    qx[pad : pad + length] = q_ref[...].astype(F32)
    qx[pad + length :] = qn_ref[...].astype(F32)
    gx[:length] = g_ref[...].astype(F32)
    gx[length:] = gn_ref[...].astype(F32)

    def taps(which):
        return [jnp.broadcast_to(sf_ref[which, i : i + 1, :], (ROWS, width)) for i in range(ntap)]

    def conv(ref, row, weights):
        window = ref[pl.ds(row - 8, ROWS + 8), :]
        total = weights[0] * window[8:]
        for i in range(1, ntap):
            total = total + weights[i] * down(window, i, ROWS)
        return total

    wk, wv, wq = taps(1), taps(2), taps(0)
    per = span // ROWS

    def make_z(c, _):
        row = pl.multiple_of(c * ROWS, ROWS)
        a = conv(kx, row + pad, wk)
        b = conv(vx, row + pad, wv)
        z = a * b
        kf[pl.ds(row, ROWS), :] = a
        vf[pl.ds(row, ROWS), :] = b
        zf[pl.ds(row, ROWS), :] = z
        return 0

    lax.fori_loop(0, (span + length + pad) // ROWS, make_z, 0, unroll=2)

    def make_g(c, _):
        row = pl.multiple_of(c * ROWS, ROWS)
        gs[pl.ds(row, ROWS), :] = gx[pl.ds(row, ROWS), :] * conv(qx, row + pad, wq)
        return 0

    lax.fori_loop(0, (length + span + pad) // ROWS, make_g, 0, unroll=2)

    def forward(block, out):
        high, low = split(block)
        stack = jnp.concatenate([high, low], 0)
        out[...] = jnp.dot(fh_ref[...], stack, preferred_element_type=F32) + jnp.dot(
            fl_ref[...], high, preferred_element_type=F32
        )

    def inverse(out):
        out[...] = (
            jnp.dot(ih_ref[...], prod[0], preferred_element_type=F32)
            + jnp.dot(ih_ref[...], prod[1], preferred_element_type=F32)
            + jnp.dot(il_ref[...], prod[0], preferred_element_type=F32)
        )

    first = lax.broadcasted_iota(jnp.int32, (span, width), 0) == 0
    forward(lf_ref[...] + jnp.where(first, gain_ref[...], 0.0), hw)

    def fwd_both(b, _):
        row = pl.multiple_of(b * span, span)
        forward(zf[pl.ds(row, span), :], zw.at[b])
        forward(gs[pl.ds(row, span), :], gw.at[b])
        return 0

    lax.fori_loop(0, nblk + 1, fwd_both, 0)
    acc[...] = jnp.zeros_like(acc)

    def point(b, _):
        row = pl.multiple_of(b * span, span)
        for c in range(span // ROWS):
            sign = 1 if c * ROWS < half else -1
            re = slice(c * ROWS, (c + 1) * ROWS)
            im = slice(span + c * ROWS, span + (c + 1) * ROWS)
            hr, hi = hw[re], hw[im]
            if sign > 0:
                yr = zw[b + 1, re] - zw[b, im]
                yi = zw[b + 1, im] + zw[b, re]
            else:
                yr = zw[b + 1, re] + zw[b, im]
                yi = zw[b + 1, im] - zw[b, re]
            gr, gi = gw[b, re], gw[b, im]
            ph, plo = split(yr * hr - yi * hi)
            prod[0, re] = ph
            prod[1, re] = plo
            ph, plo = split(yr * hi + yi * hr)
            prod[0, im] = ph
            prod[1, im] = plo
            acc[re] += gr * yr + gi * yi
            acc[im] += gi * yr - gr * yi
        inverse(sx.at[pl.ds(row, span)])
        for c in range(span // ROWS):
            sign = 1 if c * ROWS < half else -1
            re = slice(c * ROWS, (c + 1) * ROWS)
            im = slice(span + c * ROWS, span + (c + 1) * ROWS)
            hr, hi = hw[re], hw[im]
            if sign > 0:
                yr = gw[b, re] + gw[b + 1, im]
                yi = gw[b, im] - gw[b + 1, re]
            else:
                yr = gw[b, re] - gw[b + 1, im]
                yi = gw[b, im] + gw[b + 1, re]
            ph, plo = split(yr * hr + yi * hi)
            prod[0, re] = ph
            prod[1, re] = plo
            ph, plo = split(yi * hr - yr * hi)
            prod[0, im] = ph
            prod[1, im] = plo
        inverse(gz.at[pl.ds(row, span)])
        return 0

    lax.fori_loop(0, nblk, point, 0)
    for c in range(span // ROWS):
        for start in (0, span):
            rows = slice(start + c * ROWS, start + (c + 1) * ROWS)
            ph, plo = split(acc[rows])
            prod[0, rows] = ph
            prod[1, rows] = plo
    inverse(part_ref.at[:span])

    taps_h = lf_ref[...]
    back_h = hr_ref[...]
    gain = gain_ref[...]
    line = lax.broadcasted_iota(jnp.int32, (8, width), 0)
    edge_s = jnp.zeros((8, width), F32)
    edge_z = jnp.zeros((8, width), F32)
    for i in range(ntap - 1):
        zrow = zf[length + span + i : length + span + i + 1, :]
        grow = gs[length + i : length + i + 1, :]
        win = zf[length + i + 1 : length + i + 1 + span, :]
        value = jnp.sum(win * back_h, axis=0, keepdims=True) + gain * zrow
        edge_s = jnp.where(line == i, value, edge_s)
        win = gs[length + i : length + i + span, :]
        value = jnp.sum(win * taps_h, axis=0, keepdims=True) + gain * grow
        edge_z = jnp.where(line == i, value, edge_z)
    eq = gx[length : length + 8] * edge_s
    ek = edge_z * vf[length + span : length + span + 8]
    ev = edge_z * kf[length + span : length + span + 8]

    def back(grad, after, weights, out_ref, row, own, sums):
        window = jnp.concatenate([grad, after], 0)
        total = weights[0] * grad
        new = [sums[0] + fold(grad * own)]
        for i in range(1, ntap):
            later = up(window, i, ROWS)
            total = total + weights[i] * later
            new.append(sums[i] + fold(later * own))
        out_ref[pl.ds(row, ROWS), :] = total.astype(BF16)
        return grad[:8], new

    def fold(value):
        total = value[:8]
        for r in range(8, ROWS, 8):
            total = total + value[r : r + 8]
        return total

    steps = length // ROWS

    def last(c, carry):
        after, sums = carry
        row = pl.multiple_of((steps - 1 - c) * ROWS, ROWS)
        gzc = gz[pl.ds(row, ROWS), :]
        gq = gx[pl.ds(row, ROWS), :] * sx[pl.ds(row, ROWS), :]
        gk = gzc * vf[pl.ds(row + span, ROWS), :]
        gv = gzc * kf[pl.ds(row + span, ROWS), :]
        aq, s0 = back(gq, after[0], wq, bq_ref, row, qx[pl.ds(row + pad, ROWS), :], sums[0])
        ak, s1 = back(gk, after[1], wk, bk_ref, row, kx[pl.ds(row + big, ROWS), :], sums[1])
        av, s2 = back(gv, after[2], wv, bv_ref, row, vx[pl.ds(row + big, ROWS), :], sums[2])
        return (aq, ak, av), (s0, s1, s2)

    zero = [jnp.zeros((8, width), F32) for _ in range(ntap)]
    _, sums = lax.fori_loop(0, steps, last, ((eq, ek, ev), (zero, zero, zero)), unroll=2)
    rows = [jnp.sum(sums[w][i], axis=0, keepdims=True) for w in range(3) for i in range(ntap)]
    rows.append(part_ref[0:1, :])
    extra = part_ref.shape[0] - span - len(rows)
    part_ref[span:] = jnp.concatenate(rows + [jnp.zeros((extra, width), F32)], 0)


def body(input_q, input_k, input_v, grad_out, short_filters, long_filter, skip_gain):
    length, channels = input_q.shape
    ntap = short_filters.shape[1]
    span = long_filter.shape[0]
    pad = 16
    big = span + pad
    width = min(256, channels)
    kp = shifted(input_k[length - big :], "seq", 1)
    vp = shifted(input_v[length - big :], "seq", 1)
    qp = shifted(input_q[length - pad :], "seq", 1)
    qn = shifted(input_q[:big], "seq", -1)
    gn = shifted(grad_out[:big], "seq", -1)
    kn = shifted(input_k[:pad], "seq", -1)
    vn = shifted(input_v[:pad], "seq", -1)
    mats = [jnp.asarray(m) for m in transforms(span)]
    nblk = length // span

    def tile(rows):
        return pl.BlockSpec((rows, width), lambda i: (0, i))

    def whole(mat):
        return pl.BlockSpec(mat.shape, lambda i: (0, 0))

    more = -(-(3 * ntap + 1) // 8) * 8
    cells = lambda rows: pltpu.VMEM((rows, width), F32)
    ext = length + big
    back_q, back_k, back_v, part = pl.pallas_call(
        functools.partial(kernel, length, span, ntap, pad),
        grid=(channels // width,),
        out_shape=(
            jax.ShapeDtypeStruct((length, channels), BF16),
            jax.ShapeDtypeStruct((length, channels), BF16),
            jax.ShapeDtypeStruct((length, channels), BF16),
            jax.ShapeDtypeStruct((span + more, channels), F32),
        ),
        in_specs=[tile(length)] * 4
        + [tile(big), tile(big), tile(pad), tile(big), tile(big), tile(pad), tile(pad)]
        + [pl.BlockSpec((3, ntap, width), lambda i: (0, 0, i)), tile(span), tile(span), tile(1)]
        + [whole(m) for m in mats],
        out_specs=(tile(length), tile(length), tile(length), tile(span + more)),
        scratch_shapes=[
            cells(ext + pad), cells(ext + pad), cells(ext + pad), cells(ext),
            cells(ext), cells(ext), cells(ext), cells(ext),
            cells(8), cells(8),
            pltpu.VMEM((nblk + 1, 2 * span, width), F32),
            pltpu.VMEM((nblk + 1, 2 * span, width), F32),
            cells(2 * span), cells(2 * span), cells(length), cells(length),
            pltpu.VMEM((2, 2 * span, width), BF16),
        ],
        compiler_params=pltpu.CompilerParams(
            dimension_semantics=("arbitrary",), vmem_limit_bytes=56 * 1024 * 1024
        ),
        name="hyena_back",
    )(
        input_q, input_k, input_v, grad_out, kp, vp, qp, qn, gn, kn, vn,
        short_filters, long_filter, long_filter[::-1], skip_gain[None], *mats,
    )
    grad_filt = lax.psum_scatter(part[:span], "seq", scatter_dimension=0, tiled=True)
    small = lax.psum(part[span:], "seq")
    grad_taps = small[: 3 * ntap].reshape(3, ntap, channels)
    return (back_q, back_k, back_v, grad_filt, grad_taps, small[3 * ntap])


def solution(mesh):
    return jax.shard_map(
        body,
        mesh=mesh,
        in_specs=(
            P("seq", "ch"),
            P("seq", "ch"),
            P("seq", "ch"),
            P("seq", "ch"),
            P(None, None, "ch"),
            P(None, "ch"),
            P("ch"),
        ),
        out_specs=(
            P("seq", "ch"),
            P("seq", "ch"),
            P("seq", "ch"),
            P("seq", "ch"),
            P(None, None, "ch"),
            P("ch"),
        ),
        check_vma=False,
    )
```

profile of v0, /device:TPU:0, one launch (start us, length us, event | category | flops | bytes accessed | tf_op | source)
XLA Modules:
  0.0 200.3 jit_solution(17053152230927779500)
XLA Ops:
  7.2 0.0 all-reduce.2.cloned.1.call-start
  7.2 1.9 slice.34
  9.1 0.0 copy-start
  9.1 2.6 %collective-permute-start.1 = (bf16[144,2048]{1,0:T(8,128)(2,1)}, bf16[144,2048]{1,0:T(8,128)(2,1)S(1)}, u32[]{:S(2)}, u32[]{:S(2)}) collective-permute-start(bf16[144,2048]{1,0:T(8,128)(2,1)} %slice.34), channel_id=1, source_target_pairs={{0,4},{4,8},{8,12},{12,16},{16,20},{20,24},{24,28},{1,5},{5,9},{9,... | collective-permute-start | bytes 1769480 | tf_op jit(solution)/shard_map/ppermute | solution.py:19
  11.7 1.9 slice.33
  13.6 4.6 %collective-permute-start = (bf16[144,2048]{1,0:T(8,128)(2,1)}, bf16[144,2048]{1,0:T(8,128)(2,1)S(1)}, u32[]{:S(2)}, u32[]{:S(2)}) collective-permute-start(bf16[144,2048]{1,0:T(8,128)(2,1)} %slice.33), channel_id=1, source_target_pairs={{0,4},{4,8},{8,12},{12,16},{16,20},{20,24},{24,28},{1,5},{5,9},{9,... | collective-permute-start | bytes 1769480 | tf_op jit(solution)/shard_map/ppermute | solution.py:19
  18.2 1.9 slice.36
  20.2 1.3 collective-permute-start.3
  21.4 1.9 slice.37
  23.4 1.3 collective-permute-start.4
  24.7 0.8 slice.39
  25.5 1.3 collective-permute-start.6
  26.8 0.8 slice.38
  27.6 2.3 %collective-permute-done.6.vn_ref = bf16[16,2048]{1,0:T(8,128)(2,1)S(1)} collective-permute-done((bf16[16,2048]{1,0:T(8,128)(2,1)S(1)}, bf16[16,2048]{1,0:T(8,128)(2,1)S(1)}, u32[]{:S(2)}, u32[]{:S(2)}) %collective-permute-start.6) | collective-permute-done | bytes 65568 | tf_op jit(solution)/shard_map/ppermute | solution.py:19
  29.9 0.0 copy-start.5
  29.9 1.3 collective-permute-start.5
  31.2 1.5 slice.35
  32.7 8.5 %collective-permute-done.5.kn_ref = bf16[16,2048]{1,0:T(8,128)(2,1)S(1)} collective-permute-done((bf16[16,2048]{1,0:T(8,128)(2,1)S(1)}, bf16[16,2048]{1,0:T(8,128)(2,1)S(1)}, u32[]{:S(2)}, u32[]{:S(2)}) %collective-permute-start.5) | collective-permute-done | bytes 65568 | tf_op jit(solution)/shard_map/ppermute | solution.py:19
  41.2 0.0 copy-start.6
  41.2 5.4 %collective-permute-start.2 = (bf16[16,2048]{1,0:T(8,128)(2,1)}, bf16[16,2048]{1,0:T(8,128)(2,1)}, u32[]{:S(2)}, u32[]{:S(2)}) collective-permute-start(bf16[16,2048]{1,0:T(8,128)(2,1)} %slice.35), channel_id=1, source_target_pairs={{0,4},{4,8},{8,12},{12,16},{16,20},{20,24},{24,28},{1,5},{5,9},{9,... | collective-permute-start | bytes 196616 | tf_op jit(solution)/shard_map/ppermute | solution.py:19
  46.6 0.0 copy-done
  46.6 5.3 %rev.3.hr_ref = f32[128,2048]{1,0:T(8,128)} reverse(f32[128,2048]{1,0:T(8,128)S(1)} %copy-done), dimensions={0} | reverse | bytes 2097152 | tf_op jit(solution)/shard_map/rev | solution.py:304
  51.9 0.0 collective-permute-done.2.qp_ref
  51.9 0.0 collective-permute-done.1.vp_ref
  51.9 0.0 copy-start.1
  51.9 0.0 collective-permute-done.kp_ref
  51.9 0.0 copy-start.2
  52.0 0.0 collective-permute-done.3.qn_ref
  52.0 0.0 copy-start.3
  52.0 0.0 collective-permute-done.4.gn_ref
  52.0 0.0 copy-start.4
  52.0 0.0 copy-done.5
  52.0 0.0 copy-done.6
  52.0 0.7 copy-done.1
  52.7 0.2 copy-done.2
  52.9 0.2 copy-done.3
  53.1 0.2 copy-done.4
  53.3 49.2 %hyena_back.1 = (bf16[512,2048]{1,0:T(8,128)(2,1)}, bf16[512,2048]{1,0:T(8,128)(2,1)}, bf16[512,2048]{1,0:T(8,128)(2,1)}, f32[144,2048]{1,0:T(8,128)}) custom-call(bf16[512,2048]{1,0:T(8,128)(2,1)} %q_ref.1, bf16[512,2048]{1,0:T(8,128)(2,1)} %k_ref.1, bf16[512,2048]{1,0:T(8,128)(2,1)} %v_ref.1, bf16[512,2048]{1,0:T(8,128)(2,1)} %g_ref.1, ...), custom_call_target="tpu_custom_call" | custom-call | tf_op jit(solution)/shard_map/hyena_back/pallas_call | solution.py:275
  102.5 1.6 slice.41
  104.1 0.0 all-reduce.2.cloned.1.call-update
  104.1 0.0 reduce-scatter.2.cloned.1.call-start
  104.2 2.3 %slice.40 = f32[128,2048]{1,0:T(8,128)} slice(f32[144,2048]{1,0:T(8,128)} %get-tuple-element.13), slice={[0:128], [0:2048]} | slice | bytes 2097152 | tf_op jit(solution)/shard_map/slice | solution.py:306
  106.5 0.0 reduce-scatter.2.cloned.1.call-update
  106.5 52.4 %all-reduce.2.cloned.1.call-done = f32[16,2048]{1,0:T(8,128)} async-done(((f32[16,2048]{1,0:T(8,128)}), f32[16,2048]{1,0:T(8,128)}) %all-reduce.2.cloned.1.call-update) | async-done | bytes 131088 | tf_op jit(solution)/shard_map/psum | solution.py:307
  158.9 1.6 reshape.15
  160.5 1.4 slice.45
  162.0 31.6 %reduce-scatter.2.cloned.1.call-done = f32[16,2048]{1,0:T(8,128)} async-done(((f32[128,2048]{1,0:T(8,128)}), f32[16,2048]{1,0:T(8,128)}) %reduce-scatter.2.cloned.1.call-update) | async-done | bytes 131088 | tf_op jit(solution)/shard_map/reduce_scatter | solution.py:306
Async XLA Ops:
  7.2 151.8 %all-reduce.2.cloned.1.call-start = ((), (), s32[]{:S(2)}) async-start(), calls=%async_computation.2 | async-start | bytes 262144 | tf_op jit(solution)/shard_map/psum | solution.py:307
  9.1 37.5 %copy-start = (f32[128,2048]{1,0:T(8,128)S(1)}, f32[128,2048]{1,0:T(8,128)}, u32[]{:S(2)}) copy-start(f32[128,2048]{1,0:T(8,128)} %lf_ref.1) | copy-start | bytes 3145732
  9.1 42.8 %collective-permute-start.1 = (bf16[144,2048]{1,0:T(8,128)(2,1)}, bf16[144,2048]{1,0:T(8,128)(2,1)S(1)}, u32[]{:S(2)}, u32[]{:S(2)}) collective-permute-start(bf16[144,2048]{1,0:T(8,128)(2,1)} %slice.34), channel_id=1, source_target_pairs={{0,4},{4,8},{8,12},{12,16},{16,20},{20,24},{24,28},{1,5},{5,9},{9,... | collective-permute-start | bytes 1769480 | tf_op jit(solution)/shard_map/ppermute | solution.py:19
  13.6 38.3 %collective-permute-start = (bf16[144,2048]{1,0:T(8,128)(2,1)}, bf16[144,2048]{1,0:T(8,128)(2,1)S(1)}, u32[]{:S(2)}, u32[]{:S(2)}) collective-permute-start(bf16[144,2048]{1,0:T(8,128)(2,1)} %slice.33), channel_id=1, source_target_pairs={{0,4},{4,8},{8,12},{12,16},{16,20},{20,24},{24,28},{1,5},{5,9},{9,... | collective-permute-start | bytes 1769480 | tf_op jit(solution)/shard_map/ppermute | solution.py:19
  20.2 31.8 %collective-permute-start.3 = (bf16[144,2048]{1,0:T(8,128)(2,1)}, bf16[144,2048]{1,0:T(8,128)(2,1)S(1)}, u32[]{:S(2)}, u32[]{:S(2)}) collective-permute-start(bf16[144,2048]{1,0:T(8,128)(2,1)} %slice.36), channel_id=1, source_target_pairs={{4,0},{8,4},{12,8},{16,12},{20,16},{24,20},{28,24},{5,1},{9,5},{13... | collective-permute-start | bytes 1769480 | tf_op jit(solution)/shard_map/ppermute | solution.py:19
  23.4 28.6 %collective-permute-start.4 = (bf16[144,2048]{1,0:T(8,128)(2,1)}, bf16[144,2048]{1,0:T(8,128)(2,1)S(1)}, u32[]{:S(2)}, u32[]{:S(2)}) collective-permute-start(bf16[144,2048]{1,0:T(8,128)(2,1)} %slice.37), channel_id=1, source_target_pairs={{4,0},{8,4},{12,8},{16,12},{20,16},{24,20},{28,24},{5,1},{9,5},{13... | collective-permute-start | bytes 1769480 | tf_op jit(solution)/shard_map/ppermute | solution.py:19
  25.5 4.4 %collective-permute-start.6 = (bf16[16,2048]{1,0:T(8,128)(2,1)S(1)}, bf16[16,2048]{1,0:T(8,128)(2,1)S(1)}, u32[]{:S(2)}, u32[]{:S(2)}) collective-permute-start(bf16[16,2048]{1,0:T(8,128)(2,1)S(1)} %slice.39), channel_id=1, source_target_pairs={{4,0},{8,4},{12,8},{16,12},{20,16},{24,20},{28,24},{5,1},{9,5},{13... | collective-permute-start | bytes 196616 | tf_op jit(solution)/shard_map/ppermute | solution.py:19
  29.9 22.1 %copy-start.5 = (bf16[16,2048]{1,0:T(8,128)(2,1)}, bf16[16,2048]{1,0:T(8,128)(2,1)S(1)}, u32[]{:S(2)}) copy-start(bf16[16,2048]{1,0:T(8,128)(2,1)S(1)} %collective-permute-done.6.vn_ref) | copy-start | bytes 196612
  29.9 11.3 %collective-permute-start.5 = (bf16[16,2048]{1,0:T(8,128)(2,1)S(1)}, bf16[16,2048]{1,0:T(8,128)(2,1)S(1)}, u32[]{:S(2)}, u32[]{:S(2)}) collective-permute-start(bf16[16,2048]{1,0:T(8,128)(2,1)S(1)} %slice.38), channel_id=1, source_target_pairs={{4,0},{8,4},{12,8},{16,12},{20,16},{24,20},{28,24},{5,1},{9,5},{13... | collective-permute-start | bytes 196616 | tf_op jit(solution)/shard_map/ppermute | solution.py:19
  41.2 10.8 %copy-start.6 = (bf16[16,2048]{1,0:T(8,128)(2,1)}, bf16[16,2048]{1,0:T(8,128)(2,1)S(1)}, u32[]{:S(2)}) copy-start(bf16[16,2048]{1,0:T(8,128)(2,1)S(1)} %collective-permute-done.5.kn_ref) | copy-start | bytes 196612
  41.2 10.7 %collective-permute-start.2 = (bf16[16,2048]{1,0:T(8,128)(2,1)}, bf16[16,2048]{1,0:T(8,128)(2,1)}, u32[]{:S(2)}, u32[]{:S(2)}) collective-permute-start(bf16[16,2048]{1,0:T(8,128)(2,1)} %slice.35), channel_id=1, source_target_pairs={{0,4},{4,8},{8,12},{12,16},{16,20},{20,24},{24,28},{1,5},{5,9},{9,... | collective-permute-start | bytes 196616 | tf_op jit(solution)/shard_map/ppermute | solution.py:19
  51.9 0.8 copy-start.1
  51.9 1.0 copy-start.2
  52.0 1.2 copy-start.3
  52.0 1.3 copy-start.4
  104.1 89.4 %reduce-scatter.2.cloned.1.call-start = ((), (), s32[]{:S(2)}) async-start(), calls=%async_computation.1 | async-start | bytes 1179648 | tf_op jit(solution)/shard_map/reduce_scatter | solution.py:306
Sparse Core Ops, SparseCore 0:
  104.2 54.6 all-reduce.1
  161.8 31.6 reduce-scatter.1
where the time goes:
time: 201 us; the launch traced here: 200 us
  waiting for transfers between devices  94.8 us (47%)
  Pallas kernels  49.2 us (24%)
  local copies, waits for them, and re-layouts  24.4 us (12%)
  starting transfers between devices  17.8 us (9%)
  between operations  14.2 us (7%)
    psum x1, waiting for transfers between devices, body(): small = lax.psum(part[span:], 'seq')  52.4 us
    pallas_call x1, Pallas kernels, body(): pl.pallas_call(functools.partial(kernel, length, span, ntap, pad), grid=(...  49.2 us
    reduce_scatter x1, waiting for transfers between devices, body(): lax.psum_scatter(part[:span], 'seq', scatter_dimension=0, tiled=True)  31.6 us
    ppermute x7, starting transfers between devices, shifted(): return lax.ppermute(value, axis, pairs)  17.7 us
    ppermute x7, waiting for transfers between devices, shifted(): return lax.ppermute(value, axis, pairs)  10.8 us
    rev x1, local copies, waits for them, and re-layouts, body(): long_filter[::-1]  5.28 us
  transfers between devices with their start and end apart: 9, of which 4 were waited for; matrix products, arithmetic and copies ran while one was open for 10% of the time, Pallas kernels for 0%

commit v1 on v0

--- a/solution.py
+++ b/solution.py
@@ -13,12 +13,6 @@
 ROWS = 16
 
 
-def shifted(value, axis, by):
-    size = lax.axis_size(axis)
-    pairs = [(i, i + by) for i in range(size) if 0 <= i + by < size]
-    return lax.ppermute(value, axis, pairs)
-
-
 def transforms(span):
     freq = np.concatenate([np.arange(0, span, 2), np.arange(1, span, 2)]) + 0.5
     angle = np.pi * np.outer(freq, np.arange(span)) / span
@@ -38,6 +32,7 @@
         fl,
         ih,
         il,
+        np.concatenate([np.eye(span)[::-1]] * 2, 1).astype(jnp.bfloat16),
     )
 
 
@@ -55,17 +50,120 @@
     return pltpu.roll(window, rows + 8 - by, 0)[:rows]
 
 
+def remote(src, dst, send, recv, target):
+    return pltpu.make_async_remote_copy(
+        src_ref=src,
+        dst_ref=dst,
+        send_sem=send,
+        recv_sem=recv,
+        device_id={"seq": target},
+        device_id_type=pl.DeviceIdType.MESH,
+    )
+
+
 def kernel(
-    length, span, ntap, pad,
-    q_ref, k_ref, v_ref, g_ref, kp_ref, vp_ref, qp_ref, qn_ref, gn_ref, kn_ref, vn_ref,
-    sf_ref, lf_ref, hr_ref, gain_ref, fh_ref, fl_ref, ih_ref, il_ref,
-    bq_ref, bk_ref, bv_ref, part_ref,
-    qx, kx, vx, gx, kf, vf, zf, gs, zs, gss, zw, gw, hw, acc, sx, gz, prod,
+    size, length, span, ntap, pad,
+    q_ref, k_ref, v_ref, g_ref, q_all, k_all, v_all, g_all,
+    sf_ref, lf_ref, gain_ref, fh_ref, fl_ref, ih_ref, il_ref, flip_ref,
+    bq_ref, bk_ref, bv_ref, filt_ref, taps_ref, skip_ref,
+    qx, kx, vx, gx, kf, vf, zf, gs, zw, gw, hw, acc, sx, gz, prod, part,
+    kp_all, vp_all, qp_all, qn_all, gn_all, kn_all, vn_all,
+    mine, theirs, chip, others,
+    halo_send, halo_recv, pair_send, pair_recv, chip_send, chip_recv,
 ):
     width = q_ref.shape[1]
     half = span // 2
     nblk = length // span
     big = span + pad
+    tile = pl.program_id(0)
+    tiles = kp_all.shape[0]
+    chips = size // 2
+    block = span // size
+    me = lax.axis_index("seq")
+    core = lax.rem(me, 2)
+    place = me // 2
+    partner = me + 1 - 2 * core
+
+    def to_next(t):
+        cols = pl.ds(pl.multiple_of(t * width, width), width)
+        target = lax.rem(me + 1, size)
+        parts = ((k_all, big, kp_all), (v_all, big, vp_all), (q_all, pad, qp_all))
+        return [
+            remote(src.at[pl.ds(length - rows, rows), cols], dst.at[t], halo_send.at[t, j], halo_recv.at[t, j], target)
+            for j, (src, rows, dst) in enumerate(parts)
+        ]
+
+    def to_prev(t):
+        cols = pl.ds(pl.multiple_of(t * width, width), width)
+        target = lax.rem(me + size - 1, size)
+        parts = ((q_all, big, qn_all), (g_all, big, gn_all), (k_all, pad, kn_all), (v_all, pad, vn_all))
+        return [
+            remote(src.at[pl.ds(0, rows), cols], dst.at[t], halo_send.at[t, 3 + j], halo_recv.at[t, 3 + j], target)
+            for j, (src, rows, dst) in enumerate(parts)
+        ]
+
+    def pair_copy(t):
+        return remote(mine.at[t, 1 - core], theirs.at[t], pair_send.at[t], pair_recv.at[t], partner)
+
+    def chip_copy(t, d):
+        there = lax.rem(place + d, chips)
+        return remote(chip.at[t, there], others.at[t, d], chip_send.at[t, d], chip_recv.at[t, d], there * 2 + core)
+
+    @pl.when(tile == 0)
+    def _():
+        barrier = pltpu.get_barrier_semaphore()
+        for d in range(1, size):
+            pl.semaphore_signal(
+                barrier, inc=1, device_id={"seq": lax.rem(me + d, size)}, device_id_type=pl.DeviceIdType.MESH
+            )
+        pl.semaphore_wait(barrier, size - 1)
+
+        def send(t, _):
+            @pl.when(me < size - 1)
+            def _():
+                for copy in to_next(t):
+                    copy.start()
+
+            @pl.when(me > 0)
+            def _():
+                for copy in to_prev(t):
+                    copy.start()
+
+            return 0
+
+        lax.fori_loop(0, tiles, send, 0)
+
+        @pl.when(me == 0)
+        def _():
+            for ref in (kp_all, vp_all, qp_all):
+                ref[...] = jnp.zeros_like(ref)
+
+        @pl.when(me == size - 1)
+        def _():
+            for ref in (qn_all, gn_all, kn_all, vn_all):
+                ref[...] = jnp.zeros_like(ref)
+
+    @pl.when(me > 0)
+    def _():
+        for copy in to_next(tile):
+            copy.wait_recv()
+
+    @pl.when(me < size - 1)
+    def _():
+        for copy in to_prev(tile):
+            copy.wait_recv()
+
+    kp_ref, vp_ref, qp_ref = kp_all.at[tile], vp_all.at[tile], qp_all.at[tile]
+    qn_ref, gn_ref, kn_ref, vn_ref = qn_all.at[tile], gn_all.at[tile], kn_all.at[tile], vn_all.at[tile]
+
+    def join_chip(t):
+        pair_copy(t).wait_recv()
+        total = mine[t, core] + theirs[t]
+        chip[t] = total
+        others[t, 0] = mine[t, core, place] + theirs[t, place]
+        for d in range(1, chips):
+            chip_copy(t, d).start()
+
     kx[:big] = kp_ref[...].astype(F32)
     kx[big : big + length] = k_ref[...].astype(F32)
     kx[big + length :] = kn_ref[...].astype(F32)
@@ -135,6 +233,10 @@
 
     lax.fori_loop(0, nblk + 1, fwd_both, 0)
     acc[...] = jnp.zeros_like(acc)
+
+    @pl.when(tile > 0)
+    def _():
+        join_chip(tile - 1)
 
     def point(b, _):
         row = pl.multiple_of(b * span, span)
@@ -186,10 +288,10 @@
             ph, plo = split(acc[rows])
             prod[0, rows] = ph
             prod[1, rows] = plo
-    inverse(part_ref.at[:span])
+    inverse(part)
 
     taps_h = lf_ref[...]
-    back_h = hr_ref[...]
+    back_h = jnp.dot(flip_ref[...], jnp.concatenate(split(taps_h), 0), preferred_element_type=F32)
     gain = gain_ref[...]
     line = lax.broadcasted_iota(jnp.int32, (8, width), 0)
     edge_s = jnp.zeros((8, width), F32)
@@ -241,9 +343,47 @@
     zero = [jnp.zeros((8, width), F32) for _ in range(ntap)]
     _, sums = lax.fori_loop(0, steps, last, ((eq, ek, ev), (zero, zero, zero)), unroll=2)
     rows = [jnp.sum(sums[w][i], axis=0, keepdims=True) for w in range(3) for i in range(ntap)]
-    rows.append(part_ref[0:1, :])
-    extra = part_ref.shape[0] - span - len(rows)
-    part_ref[span:] = jnp.concatenate(rows + [jnp.zeros((extra, width), F32)], 0)
+    rows.append(part[0:1, :])
+    small = jnp.concatenate(rows + [jnp.zeros((pad - len(rows), width), F32)], 0)
+    for d in range(size):
+        mine[tile, d % 2, d // 2, :block] = part[d * block : (d + 1) * block]
+        mine[tile, d % 2, d // 2, block:] = small
+    pair_copy(tile).start()
+
+    @pl.when(tile == tiles - 1)
+    def _():
+        join_chip(tiles - 1)
+
+        def finish(t, _):
+            cols = pl.ds(pl.multiple_of(t * width, width), width)
+
+            @pl.when(me < size - 1)
+            def _():
+                for copy in to_next(t):
+                    copy.wait_send()
+
+            @pl.when(me > 0)
+            def _():
+                for copy in to_prev(t):
+                    copy.wait_send()
+
+            pair_copy(t).wait_send()
+            for d in range(1, chips):
+                chip_copy(t, d).wait_send()
+                chip_copy(t, d).wait_recv()
+            total = others[t, place]
+            for z in range(1, chips):
+                total = total + others[t, lax.rem(place + chips - z, chips)]
+            filt_ref[:, cols] = total[:block]
+            for w in range(3):
+                for i in range(ntap):
+                    at = block + w * ntap + i
+                    taps_ref[w, i : i + 1, cols] = total[at : at + 1]
+            at = block + 3 * ntap
+            skip_ref[:, cols] = total[at : at + 1]
+            return 0
+
+        lax.fori_loop(0, tiles, finish, 0)
 
 
 def body(input_q, input_k, input_v, grad_out, short_filters, long_filter, skip_gain):
@@ -253,13 +393,6 @@
     pad = 16
     big = span + pad
     width = min(256, channels)
-    kp = shifted(input_k[length - big :], "seq", 1)
-    vp = shifted(input_v[length - big :], "seq", 1)
-    qp = shifted(input_q[length - pad :], "seq", 1)
-    qn = shifted(input_q[:big], "seq", -1)
-    gn = shifted(grad_out[:big], "seq", -1)
-    kn = shifted(input_k[:pad], "seq", -1)
-    vn = shifted(input_v[:pad], "seq", -1)
     mats = [jnp.asarray(m) for m in transforms(span)]
     nblk = length // span
 
@@ -269,44 +402,59 @@
     def whole(mat):
         return pl.BlockSpec(mat.shape, lambda i: (0, 0))
 
-    more = -(-(3 * ntap + 1) // 8) * 8
-    cells = lambda rows: pltpu.VMEM((rows, width), F32)
+    size = lax.axis_size("seq")
+    tiles = channels // width
+    chips = size // 2
+    block = span // size
+    cells = lambda *rows: pltpu.VMEM((*rows, width), F32)
+    edge = lambda rows: pltpu.VMEM((tiles, rows, width), BF16)
     ext = length + big
-    back_q, back_k, back_v, part = pl.pallas_call(
-        functools.partial(kernel, length, span, ntap, pad),
-        grid=(channels // width,),
+    full = pl.BlockSpec(memory_space=pl.ANY)
+    out = jax.ShapeDtypeStruct((length, channels), BF16)
+    back_q, back_k, back_v, grad_filt, grad_taps, grad_gain = pl.pallas_call(
+        functools.partial(kernel, size, length, span, ntap, pad),
+        grid=(tiles,),
         out_shape=(
-            jax.ShapeDtypeStruct((length, channels), BF16),
-            jax.ShapeDtypeStruct((length, channels), BF16),
-            jax.ShapeDtypeStruct((length, channels), BF16),
-            jax.ShapeDtypeStruct((span + more, channels), F32),
+            out, out, out,
+            jax.ShapeDtypeStruct((block, channels), F32),
+            jax.ShapeDtypeStruct((3, ntap, channels), F32),
+            jax.ShapeDtypeStruct((1, channels), F32),
         ),
         in_specs=[tile(length)] * 4
-        + [tile(big), tile(big), tile(pad), tile(big), tile(big), tile(pad), tile(pad)]
-        + [pl.BlockSpec((3, ntap, width), lambda i: (0, 0, i)), tile(span), tile(span), tile(1)]
+        + [full] * 4
+        + [pl.BlockSpec((3, ntap, width), lambda i: (0, 0, i)), tile(span), tile(1)]
         + [whole(m) for m in mats],
-        out_specs=(tile(length), tile(length), tile(length), tile(span + more)),
+        out_specs=(
+            tile(length), tile(length), tile(length),
+            pl.BlockSpec((block, channels), lambda i: (0, 0)),
+            pl.BlockSpec((3, ntap, channels), lambda i: (0, 0, 0)),
+            pl.BlockSpec((1, channels), lambda i: (0, 0)),
+        ),
         scratch_shapes=[
             cells(ext + pad), cells(ext + pad), cells(ext + pad), cells(ext),
             cells(ext), cells(ext), cells(ext), cells(ext),
-            cells(8), cells(8),
-            pltpu.VMEM((nblk + 1, 2 * span, width), F32),
-            pltpu.VMEM((nblk + 1, 2 * span, width), F32),
+            cells(nblk + 1, 2 * span), cells(nblk + 1, 2 * span),
             cells(2 * span), cells(2 * span), cells(length), cells(length),
-            pltpu.VMEM((2, 2 * span, width), BF16),
+            pltpu.VMEM((2, 2 * span, width), BF16), cells(span),
+            edge(big), edge(big), edge(pad), edge(big), edge(big), edge(pad), edge(pad),
+            cells(tiles, 2, chips, block + pad), cells(tiles, chips, block + pad),
+            cells(tiles, chips, block + pad), cells(tiles, chips, block + pad),
+            pltpu.SemaphoreType.DMA((tiles, 7)), pltpu.SemaphoreType.DMA((tiles, 7)),
+            pltpu.SemaphoreType.DMA((tiles,)), pltpu.SemaphoreType.DMA((tiles,)),
+            pltpu.SemaphoreType.DMA((tiles, chips)), pltpu.SemaphoreType.DMA((tiles, chips)),
         ],
         compiler_params=pltpu.CompilerParams(
-            dimension_semantics=("arbitrary",), vmem_limit_bytes=56 * 1024 * 1024
+            dimension_semantics=("arbitrary",),
+            vmem_limit_bytes=56 * 1024 * 1024,
+            collective_id=0,
+            has_side_effects=True,
         ),
         name="hyena_back",
     )(
-        input_q, input_k, input_v, grad_out, kp, vp, qp, qn, gn, kn, vn,
-        short_filters, long_filter, long_filter[::-1], skip_gain[None], *mats,
+        input_q, input_k, input_v, grad_out, input_q, input_k, input_v, grad_out,
+        short_filters, long_filter, skip_gain[None], *mats,
     )
-    grad_filt = lax.psum_scatter(part[:span], "seq", scatter_dimension=0, tiled=True)
-    small = lax.psum(part[span:], "seq")
-    grad_taps = small[: 3 * ntap].reshape(3, ntap, channels)
-    return (back_q, back_k, back_v, grad_filt, grad_taps, small[3 * ntap])
+    return (back_q, back_k, back_v, grad_filt, grad_taps, grad_gain[0])
 
 
 def solution(mesh):

time: 201 us -> 75.8 us (0.38)
  waiting for transfers between devices: 94.8 us -> 0 us
  starting transfers between devices: 17.8 us -> 0 us
  Pallas kernels: 49.2 us -> 66.1 us
  local copies, waits for them, and re-layouts: 24.4 us -> 8.88 us
  between operations: 14.2 us -> 0.66 us
    psum x1 -> x0, waiting for transfers between devices: 52.4 us -> none  [body(): small = lax.psum(part[span:], 'seq')]
    reduce_scatter x1 -> x0, waiting for transfers between devices: 31.6 us -> none  [body(): lax.psum_scatter(part[:span], 'seq', scatter_dimension=0, tiled=True)]
    ppermute x7 -> x0, starting transfers between devices: 17.7 us -> none  [shifted(): return lax.ppermute(value, axis, pairs)]
    pallas_call x1, Pallas kernels: 49.2 us -> 66.1 us  [body(): pl.pallas_call(functools.partial(kernel, size, length, span, ntap, pad),...]
    slice x10 -> x0, local copies, waits for them, and re-layouts: 16.2 us -> none  [the longest x1 2.29 us: body(): part[:span]]
    ppermute x7 -> x0, waiting for transfers between devices: 10.8 us -> none  [shifted(): return lax.ppermute(value, axis, pairs)]
    unnamed x14 -> x16, local copies, waits for them, and re-layouts: 1.33 us -> 8.88 us
    rev x1 -> x0, local copies, waits for them, and re-layouts: 5.28 us -> none  [body(): long_filter[::-1]]
  transfers between devices with their start and end apart: 9 -> 0, of which waited for: 4 -> 0; matrix products, arithmetic and copies ran while one was open for 10% -> 0% of each run, Pallas kernels for 0% -> 0%
where the time goes in v1:
time: 75.8 us; the launch traced here: 75.6 us
  Pallas kernels  66.1 us (87%)
  local copies, waits for them, and re-layouts  8.88 us (12%)
    pallas_call x1, Pallas kernels, body(): pl.pallas_call(functools.partial(kernel, size, length, span, ntap, pad),...  66.1 us
    unnamed x16, local copies, waits for them, and re-layouts  8.88 us

profile of v1, /device:TPU:0, one launch (start us, length us, event | category | flops | bytes accessed | tf_op | source)
XLA Modules:
  0.0 75.6 jit_solution(13972481826109857231)
XLA Ops:
  0.6 66.1 %hyena_back.1 = (bf16[512,2048]{1,0:T(8,128)(2,1)}, bf16[512,2048]{1,0:T(8,128)(2,1)}, bf16[512,2048]{1,0:T(8,128)(2,1)}, f32[16,2048]{1,0:T(8,128)}, f32[3,3,2048]{2,1,0:T(4,128)}, /*index=5*/f32[1,2048]{1,0:T(1,128)}) custom-call(bf16[512,2048]{1,0:T(8,128)(2,1)} %q_all.1, bf16[512,2048]{1,0:T(8,128)(2,1)} %k_all.1, bf16[512,2048]{1,0:T(8,128)(2,1)} %v_all.1, ...), custom_call_target="tpu_custom_call" | custom-call | tf_op jit(solution)/shard_map/hyena_back/pallas_call | solution.py:414
  66.7 0.0 copy-start.1
  66.7 3.3 %copy.24 = bf16[512,2048]{1,0:T(8,128)(2,1)} copy(bf16[512,2048]{1,0:T(8,128)(2,1)} %get-tuple-element.24) | data formatting | bytes 4194304
  70.1 0.0 copy-done.1
  70.1 0.0 copy-start
  70.1 1.3 %copy.25 = bf16[512,2048]{1,0:T(8,128)(2,1)} copy(bf16[512,2048]{1,0:T(8,128)(2,1)S(1)} %copy-done.1) | data formatting | bytes 4194304
  71.4 1.0 %copy-done = bf16[512,2048]{1,0:T(8,128)(2,1)S(1)} copy-done((bf16[512,2048]{1,0:T(8,128)(2,1)S(1)}, bf16[512,2048]{1,0:T(8,128)(2,1)}, u32[]{:S(2)}) %copy-start) | copy-done | bytes 2097176
  72.4 0.0 copy-start.2
  72.4 0.0 copy-start.3
  72.4 0.0 copy-start.4
  72.4 1.3 %copy.26 = bf16[512,2048]{1,0:T(8,128)(2,1)} copy(bf16[512,2048]{1,0:T(8,128)(2,1)S(1)} %copy-done) | data formatting | bytes 4194304
  73.7 0.0 copy-done.2
  73.7 0.7 copy.27
  74.4 0.0 copy-done.3
  74.4 0.6 copy.28
  75.0 0.0 copy-done.4
  75.0 0.6 copy.29
Async XLA Ops:
  66.7 3.3 %copy-start.1 = (bf16[512,2048]{1,0:T(8,128)(2,1)S(1)}, bf16[512,2048]{1,0:T(8,128)(2,1)}, u32[]{:S(2)}) copy-start(bf16[512,2048]{1,0:T(8,128)(2,1)} %get-tuple-element.25) | copy-start | bytes 6291460
  70.1 2.3 %copy-start = (bf16[512,2048]{1,0:T(8,128)(2,1)S(1)}, bf16[512,2048]{1,0:T(8,128)(2,1)}, u32[]{:S(2)}) copy-start(bf16[512,2048]{1,0:T(8,128)(2,1)} %get-tuple-element.26) | copy-start | bytes 6291460
  72.4 1.3 %copy-start.2 = (f32[16,2048]{1,0:T(8,128)S(1)}, f32[16,2048]{1,0:T(8,128)}, u32[]{:S(2)}) copy-start(f32[16,2048]{1,0:T(8,128)} %get-tuple-element.27) | copy-start | bytes 393220
  72.4 2.0 %copy-start.3 = (f32[3,3,2048]{2,1,0:T(4,128)S(1)}, f32[3,3,2048]{2,1,0:T(4,128)}, u32[]{:S(2)}) copy-start(f32[3,3,2048]{2,1,0:T(4,128)} %get-tuple-element.28) | copy-start | bytes 221188
  72.4 2.6 %copy-start.4 = (f32[1,2048]{1,0:T(1,128)S(1)}, f32[1,2048]{1,0:T(1,128)}, u32[]{:S(2)}) copy-start(f32[1,2048]{1,0:T(1,128)} %get-tuple-element.17) | copy-start | bytes 24580

commit v2 on v1

--- a/solution.py
+++ b/solution.py
@@ -28,10 +28,8 @@
     fh, fl = halves(fwd)
     ih, il = halves(inv)
     return (
-        np.concatenate([fh, fh], 1),
-        fl,
-        ih,
-        il,
+        np.concatenate([fh, fh, fl], 1),
+        np.concatenate([ih, ih, il], 1),
         np.concatenate([np.eye(span)[::-1]] * 2, 1).astype(jnp.bfloat16),
     )
 
@@ -64,7 +62,7 @@
 def kernel(
     size, length, span, ntap, pad,
     q_ref, k_ref, v_ref, g_ref, q_all, k_all, v_all, g_all,
-    sf_ref, lf_ref, gain_ref, fh_ref, fl_ref, ih_ref, il_ref, flip_ref,
+    sf_ref, lf_ref, gain_ref, fh_ref, ih_ref, flip_ref,
     bq_ref, bk_ref, bv_ref, filt_ref, taps_ref, skip_ref,
     qx, kx, vx, gx, kf, vf, zf, gs, zw, gw, hw, acc, sx, gz, prod, part,
     kp_all, vp_all, qp_all, qn_all, gn_all, kn_all, vn_all,
@@ -143,16 +141,6 @@
             for ref in (qn_all, gn_all, kn_all, vn_all):
                 ref[...] = jnp.zeros_like(ref)
 
-    @pl.when(me > 0)
-    def _():
-        for copy in to_next(tile):
-            copy.wait_recv()
-
-    @pl.when(me < size - 1)
-    def _():
-        for copy in to_prev(tile):
-            copy.wait_recv()
-
     kp_ref, vp_ref, qp_ref = kp_all.at[tile], vp_all.at[tile], qp_all.at[tile]
     qn_ref, gn_ref, kn_ref, vn_ref = qn_all.at[tile], gn_all.at[tile], kn_all.at[tile], vn_all.at[tile]
 
@@ -164,17 +152,10 @@
         for d in range(1, chips):
             chip_copy(t, d).start()
 
-    kx[:big] = kp_ref[...].astype(F32)
     kx[big : big + length] = k_ref[...].astype(F32)
-    kx[big + length :] = kn_ref[...].astype(F32)
-    vx[:big] = vp_ref[...].astype(F32)
     vx[big : big + length] = v_ref[...].astype(F32)
-    vx[big + length :] = vn_ref[...].astype(F32)
-    qx[:pad] = qp_ref[...].astype(F32)
     qx[pad : pad + length] = q_ref[...].astype(F32)
-    qx[pad + length :] = qn_ref[...].astype(F32)
     gx[:length] = g_ref[...].astype(F32)
-    gx[length:] = gn_ref[...].astype(F32)
 
     def taps(which):
         return [jnp.broadcast_to(sf_ref[which, i : i + 1, :], (ROWS, width)) for i in range(ntap)]
@@ -199,47 +180,60 @@
         zf[pl.ds(row, ROWS), :] = z
         return 0
 
-    lax.fori_loop(0, (span + length + pad) // ROWS, make_z, 0, unroll=2)
+    lax.fori_loop(per + 1, (span + length) // ROWS, make_z, 0, unroll=2)
 
     def make_g(c, _):
         row = pl.multiple_of(c * ROWS, ROWS)
         gs[pl.ds(row, ROWS), :] = gx[pl.ds(row, ROWS), :] * conv(qx, row + pad, wq)
         return 0
 
-    lax.fori_loop(0, (length + span + pad) // ROWS, make_g, 0, unroll=2)
+    lax.fori_loop(1, length // ROWS, make_g, 0, unroll=2)
 
     def forward(block, out):
         high, low = split(block)
-        stack = jnp.concatenate([high, low], 0)
-        out[...] = jnp.dot(fh_ref[...], stack, preferred_element_type=F32) + jnp.dot(
-            fl_ref[...], high, preferred_element_type=F32
-        )
-
-    def inverse(out):
-        out[...] = (
-            jnp.dot(ih_ref[...], prod[0], preferred_element_type=F32)
-            + jnp.dot(ih_ref[...], prod[1], preferred_element_type=F32)
-            + jnp.dot(il_ref[...], prod[0], preferred_element_type=F32)
-        )
+        stack = jnp.concatenate([high, low, high], 0)
+        out[...] = jnp.dot(fh_ref[...], stack, preferred_element_type=F32)
+
+    def inverse(at, out):
+        stack = jnp.concatenate([prod[at, 0], prod[at, 1], prod[at, 0]], 0)
+        out[...] = jnp.dot(ih_ref[...], stack, preferred_element_type=F32)
 
     first = lax.broadcasted_iota(jnp.int32, (span, width), 0) == 0
     forward(lf_ref[...] + jnp.where(first, gain_ref[...], 0.0), hw)
 
-    def fwd_both(b, _):
-        row = pl.multiple_of(b * span, span)
-        forward(zf[pl.ds(row, span), :], zw.at[b])
-        forward(gs[pl.ds(row, span), :], gw.at[b])
-        return 0
-
-    lax.fori_loop(0, nblk + 1, fwd_both, 0)
+    @pl.when(me > 0)
+    def _():
+        for copy in to_next(tile):
+            copy.wait_recv()
+
+    @pl.when(me < size - 1)
+    def _():
+        for copy in to_prev(tile):
+            copy.wait_recv()
+
+    kx[:big] = kp_ref[...].astype(F32)
+    kx[big + length :] = kn_ref[...].astype(F32)
+    vx[:big] = vp_ref[...].astype(F32)
+    vx[big + length :] = vn_ref[...].astype(F32)
+    qx[:pad] = qp_ref[...].astype(F32)
+    qx[pad + length :] = qn_ref[...].astype(F32)
+    gx[length:] = gn_ref[...].astype(F32)
+    lax.fori_loop(0, per + 1, make_z, 0, unroll=2)
+    make_z((span + length) // ROWS, 0)
+    make_g(0, 0)
+    lax.fori_loop(length // ROWS, (length + span + pad) // ROWS, make_g, 0, unroll=2)
+
+    for b in range(nblk + 1):
+        forward(zf[b * span : (b + 1) * span, :], zw.at[b])
+        forward(gs[b * span : (b + 1) * span, :], gw.at[b])
     acc[...] = jnp.zeros_like(acc)
 
     @pl.when(tile > 0)
     def _():
         join_chip(tile - 1)
 
-    def point(b, _):
-        row = pl.multiple_of(b * span, span)
+    for b in range(nblk):
+        row = b * span
         for c in range(span // ROWS):
             sign = 1 if c * ROWS < half else -1
             re = slice(c * ROWS, (c + 1) * ROWS)
@@ -253,14 +247,14 @@
                 yi = zw[b + 1, im] - zw[b, re]
             gr, gi = gw[b, re], gw[b, im]
             ph, plo = split(yr * hr - yi * hi)
-            prod[0, re] = ph
-            prod[1, re] = plo
+            prod[2 * b, 0, re] = ph
+            prod[2 * b, 1, re] = plo
             ph, plo = split(yr * hi + yi * hr)
-            prod[0, im] = ph
-            prod[1, im] = plo
+            prod[2 * b, 0, im] = ph
+            prod[2 * b, 1, im] = plo
             acc[re] += gr * yr + gi * yi
             acc[im] += gi * yr - gr * yi
-        inverse(sx.at[pl.ds(row, span)])
+        inverse(2 * b, sx.at[pl.ds(row, span)])
         for c in range(span // ROWS):
             sign = 1 if c * ROWS < half else -1
             re = slice(c * ROWS, (c + 1) * ROWS)
@@ -273,22 +267,19 @@
                 yr = gw[b, re] - gw[b + 1, im]
                 yi = gw[b, im] + gw[b + 1, re]
             ph, plo = split(yr * hr + yi * hi)
-            prod[0, re] = ph
-            prod[1, re] = plo
+            prod[2 * b + 1, 0, re] = ph
+            prod[2 * b + 1, 1, re] = plo
             ph, plo = split(yi * hr - yr * hi)
-            prod[0, im] = ph
-            prod[1, im] = plo
-        inverse(gz.at[pl.ds(row, span)])
-        return 0
-
-    lax.fori_loop(0, nblk, point, 0)
+            prod[2 * b + 1, 0, im] = ph
+            prod[2 * b + 1, 1, im] = plo
+        inverse(2 * b + 1, gz.at[pl.ds(row, span)])
     for c in range(span // ROWS):
         for start in (0, span):
             rows = slice(start + c * ROWS, start + (c + 1) * ROWS)
             ph, plo = split(acc[rows])
-            prod[0, rows] = ph
-            prod[1, rows] = plo
-    inverse(part)
+            prod[2 * nblk, 0, rows] = ph
+            prod[2 * nblk, 1, rows] = plo
+    inverse(2 * nblk, part)
 
     taps_h = lf_ref[...]
     back_h = jnp.dot(flip_ref[...], jnp.concatenate(split(taps_h), 0), preferred_element_type=F32)
@@ -435,7 +426,7 @@
             cells(ext), cells(ext), cells(ext), cells(ext),
             cells(nblk + 1, 2 * span), cells(nblk + 1, 2 * span),
             cells(2 * span), cells(2 * span), cells(length), cells(length),
-            pltpu.VMEM((2, 2 * span, width), BF16), cells(span),
+            pltpu.VMEM((2 * nblk + 1, 2, 2 * span, width), BF16), cells(span),
             edge(big), edge(big), edge(pad), edge(big), edge(big), edge(pad), edge(pad),
             cells(tiles, 2, chips, block + pad), cells(tiles, chips, block + pad),
             cells(tiles, chips, block + pad), cells(tiles, chips, block + pad),

time: 75.8 us -> 64 us (0.84)
  Pallas kernels: 66.1 us -> 54.3 us
    pallas_call x1, Pallas kernels: 66.1 us -> 54.3 us  [body(): pl.pallas_call(functools.partial(kernel, size, length, span, ntap, pad),...]
where the time goes in v2:
time: 64 us; the launch traced here: 63.8 us
  Pallas kernels  54.3 us (85%)
  local copies, waits for them, and re-layouts  8.88 us (14%)
  between operations  0.66 us (1%)
    pallas_call x1, Pallas kernels, body(): pl.pallas_call(functools.partial(kernel, size, length, span, ntap, pad),...  54.3 us
    unnamed x16, local copies, waits for them, and re-layouts  8.88 us

profile of v2, /device:TPU:0, one launch (start us, length us, event | category | flops | bytes accessed | tf_op | source)
XLA Modules:
  0.0 63.8 jit_solution(10449737088222387388)
XLA Ops:
  0.6 54.3 %hyena_back.1 = (bf16[512,2048]{1,0:T(8,128)(2,1)}, bf16[512,2048]{1,0:T(8,128)(2,1)}, bf16[512,2048]{1,0:T(8,128)(2,1)}, f32[16,2048]{1,0:T(8,128)}, f32[3,3,2048]{2,1,0:T(4,128)}, /*index=5*/f32[1,2048]{1,0:T(1,128)}) custom-call(bf16[512,2048]{1,0:T(8,128)(2,1)} %q_all.1, bf16[512,2048]{1,0:T(8,128)(2,1)} %k_all.1, bf16[512,2048]{1,0:T(8,128)(2,1)} %v_all.1, ...), custom_call_target="tpu_custom_call" | custom-call | tf_op jit(solution)/shard_map/hyena_back/pallas_call | solution.py:405
  54.9 0.0 copy-start.1
  54.9 3.3 %copy.22 = bf16[512,2048]{1,0:T(8,128)(2,1)} copy(bf16[512,2048]{1,0:T(8,128)(2,1)} %get-tuple-element.24) | data formatting | bytes 4194304
  58.2 0.0 copy-done.1
  58.2 0.0 copy-start
  58.2 1.3 %copy.23 = bf16[512,2048]{1,0:T(8,128)(2,1)} copy(bf16[512,2048]{1,0:T(8,128)(2,1)S(1)} %copy-done.1) | data formatting | bytes 4194304
  59.6 1.0 %copy-done = bf16[512,2048]{1,0:T(8,128)(2,1)S(1)} copy-done((bf16[512,2048]{1,0:T(8,128)(2,1)S(1)}, bf16[512,2048]{1,0:T(8,128)(2,1)}, u32[]{:S(2)}) %copy-start) | copy-done | bytes 2097176
  60.6 0.0 copy-start.2
  60.6 0.0 copy-start.3
  60.6 0.0 copy-start.4
  60.6 1.3 %copy.24 = bf16[512,2048]{1,0:T(8,128)(2,1)} copy(bf16[512,2048]{1,0:T(8,128)(2,1)S(1)} %copy-done) | data formatting | bytes 4194304
  61.9 0.0 copy-done.2
  61.9 0.7 %copy.25 = f32[16,2048]{1,0:T(8,128)} copy(f32[16,2048]{1,0:T(8,128)S(1)} %copy-done.2) | data formatting | bytes 262144
  62.6 0.0 copy-done.3
  62.6 0.6 %copy.26 = f32[3,3,2048]{2,1,0:T(4,128)} copy(f32[3,3,2048]{2,1,0:T(4,128)S(1)} %copy-done.3) | data formatting | bytes 147456
  63.2 0.0 copy-done.4
  63.2 0.6 copy.27
Async XLA Ops:
  54.9 3.3 %copy-start.1 = (bf16[512,2048]{1,0:T(8,128)(2,1)S(1)}, bf16[512,2048]{1,0:T(8,128)(2,1)}, u32[]{:S(2)}) copy-start(bf16[512,2048]{1,0:T(8,128)(2,1)} %get-tuple-element.25) | copy-start | bytes 6291460
  58.2 2.3 %copy-start = (bf16[512,2048]{1,0:T(8,128)(2,1)S(1)}, bf16[512,2048]{1,0:T(8,128)(2,1)}, u32[]{:S(2)}) copy-start(bf16[512,2048]{1,0:T(8,128)(2,1)} %get-tuple-element.26) | copy-start | bytes 6291460
  60.6 1.3 %copy-start.2 = (f32[16,2048]{1,0:T(8,128)S(1)}, f32[16,2048]{1,0:T(8,128)}, u32[]{:S(2)}) copy-start(f32[16,2048]{1,0:T(8,128)} %get-tuple-element.27) | copy-start | bytes 393220
  60.6 2.0 %copy-start.3 = (f32[3,3,2048]{2,1,0:T(4,128)S(1)}, f32[3,3,2048]{2,1,0:T(4,128)}, u32[]{:S(2)}) copy-start(f32[3,3,2048]{2,1,0:T(4,128)} %get-tuple-element.28) | copy-start | bytes 221188
  60.6 2.6 %copy-start.4 = (f32[1,2048]{1,0:T(1,128)S(1)}, f32[1,2048]{1,0:T(1,128)}, u32[]{:S(2)}) copy-start(f32[1,2048]{1,0:T(1,128)} %get-tuple-element.17) | copy-start | bytes 24580
